TPU v7x, 32 devices: a whole 2x2x4 slice. The times are simulated.
32 devices in a mesh: ctx: 8 (over z, y), head: 4 (over x, core).
Axes of the slice: x: 2, y: 2, z: 4, core: 2. Of those that a mesh axis runs over, the one named last changes fastest.
Arguments:
- queries: bfloat16 [8192, 16, 128], P('ctx', 'head'), may hold values from -240 to 240, as said below
- lookup_arrays: bfloat16 [8192, 4, 128], P('ctx', 'head'), may hold values from -6 to 6
- content_arrays: bfloat16 [8192, 4, 128], P('ctx', 'head'), may hold values from -6 to 6
- selection: int32 [16, 4, 6], P('ctx', 'head'), may hold values from 0 to 15, as said below
- final_mapping: bfloat16 [2048, 4096], P('head'), may hold values from -0.125 to 0.125
Outputs:
- layer_out: bfloat16 [8192, 4096], P(('ctx', 'head'))
Inputs may be any that keep to these rules, and one draw needn't show every extreme that they name: `queries`: entries lie within -240 and 240. selection[b, h, :] holds 6 block numbers no larger than b; those smaller than b are distinct, and an entry equal to b names nothing. For each KV head and each index c of ctx, the selections of the 2 blocks held at c name, among the blocks held at any one index below c, at most one distinct block, and this bound is met.
All inputs are finite; a program needn't handle non-finite values.
Results may differ from a plain program's by a relative error of at most 0.01.
Values may be sent and summed in bfloat16 or wider, within the bound.
A program may use at most 128 MiB of HBM per device.

v0:
```python
import jax
import jax.numpy as jnp
from jax import lax
from jax.sharding import PartitionSpec as P


def attend_block(operands):
    query_block, key_block, value_block, permitted_mask = operands
    block_size = query_block.shape[0]
    scaling = query_block.shape[-1] ** (-0.5)
    affinity_grid = (
        jnp.einsum("qgd,skd->gqsk", query_block, key_block, preferred_element_type=jnp.float32)
        * scaling
    )
    causal = jnp.arange(block_size)[:, None] >= jnp.arange(block_size)[None, :]
    slot_count = key_block.shape[0]
    own_slot = jnp.arange(slot_count) == slot_count - 1
    allowed = permitted_mask[:, None, None] & (~own_slot[:, None, None] | causal[None])
    allowed = allowed.transpose(1, 0, 2)[None]
    affinity_grid = jnp.where(allowed, affinity_grid, -jnp.inf)
    row_peak = jnp.max(affinity_grid, axis=(2, 3), keepdims=True)
    weights = jnp.exp(affinity_grid - row_peak)
    totals = jnp.sum(weights, axis=(2, 3))
    mixed_result = jnp.einsum(
        "gqsk,skd->qgd",
        weights.astype(jnp.bfloat16),
        value_block,
        preferred_element_type=jnp.float32,
    )
    return (mixed_result / totals.T[:, :, None]).astype(jnp.bfloat16)


def body(queries, lookup_arrays, content_arrays, selection, final_mapping):
    ctx_count = lax.axis_size("ctx")
    position = lax.axis_index("ctx")
    blocks_here = selection.shape[0]
    tokens_here = queries.shape[0]
    block_size = tokens_here // blocks_here
    askers_per_leader = queries.shape[1]
    head_dim = queries.shape[2]
    stacked = jnp.stack(
        [
            lookup_arrays.reshape(blocks_here, block_size, head_dim),
            content_arrays.reshape(blocks_here, block_size, head_dim),
        ]
    )
    chosen = selection[:, 0, :]
    holder_list = chosen // blocks_here
    distant = holder_list <= position - 1
    peer_ids = jnp.arange(ctx_count, dtype=jnp.int32)
    last_id = ctx_count * blocks_here - 1
    matches = distant[:, :, None] & (holder_list[:, :, None] == peer_ids[None, None, :])
    wanted_ids = jnp.max(jnp.where(matches, chosen[:, :, None], -1), axis=(0, 1))
    coded = jnp.where(wanted_ids >= 0, last_id - wanted_ids, -1).astype(jnp.int32)
    received = lax.all_to_all(
        coded.reshape(ctx_count, 1), "ctx", split_axis=0, concat_axis=0, tiled=True
    ).reshape(ctx_count)
    requested = last_id - received
    local_index = jnp.clip(requested - position * blocks_here, 0, blocks_here - 1)
    packed = jnp.take(stacked, local_index, axis=1)
    arrived = lax.all_to_all(packed, "ctx", split_axis=1, concat_axis=1, tiled=True)
    block_pool = jnp.concatenate([stacked, arrived], axis=1)
    block_ids = position * blocks_here + jnp.arange(blocks_here, dtype=jnp.int32)
    slot_ids = jnp.concatenate([chosen, block_ids[:, None]], axis=1)
    permitted_mask = jnp.concatenate(
        [chosen != block_ids[:, None], jnp.ones((blocks_here, 1), jnp.bool_)], axis=1
    )
    slot_owner = slot_ids // blocks_here
    pool_index = jnp.where(
        slot_owner == position, slot_ids - position * blocks_here, blocks_here + slot_owner
    )
    selected = jnp.take(block_pool, pool_index, axis=1)
    asking_lines = queries.reshape(blocks_here, block_size, askers_per_leader, head_dim)
    mixed_result = lax.map(attend_block, (asking_lines, selected[0], selected[1], permitted_mask))
    flat_rows = mixed_result.reshape(tokens_here, askers_per_leader * head_dim)

    def project():
        part_rows = lax.slice_in_dim(
            flat_rows, 0, lax.axis_size("head") * (tokens_here // lax.axis_size("head")), axis=0
        )
        return jnp.dot(part_rows, final_mapping, preferred_element_type=jnp.float32)

    summed = lax.psum_scatter(
        project().astype(jnp.bfloat16), "head", scatter_dimension=0, tiled=True
    ).astype(jnp.float32)
    return summed.astype(jnp.bfloat16)


def solution(mesh):
    in_specs = (
        P("ctx", "head", None),
        P("ctx", "head", None),
        P("ctx", "head", None),
        P("ctx", "head", None),
        P("head", None),
    )
    out_specs = P(("ctx", "head"), None)
    return jax.shard_map(body, mesh=mesh, in_specs=in_specs, out_specs=out_specs, check_vma=False)
```

profile of v0, /device:TPU:0, one launch (start us, length us, event | category | flops | bytes accessed | tf_op | source)
XLA Modules:
  0.0 254.2 jit_solution(15843986675841685980)
XLA Ops:
  6.5 0.8 copy.48
  7.3 0.8 broadcast_compare_fusion.1
  8.4 0.7 copy.49
  9.0 7.3 %all-to-all-start = ((s32[8,1,1]{2,1,0:T(1,128)}), s32[8,1,1]{2,1,0:T(1,128)S(1)}, u32[]{:S(2)}, u32[]{:S(2)}) async-start(s32[8,1,1]{2,1,0:T(1,128)} %copy.49), calls=%async_computation | async-start | bytes 8192 | tf_op jit(solution)/shard_map/all_to_all | solution.py:55
  16.4 1.1 pad_maximum_fusion.1
  17.5 5.3 %all-to-all-done = s32[8,1,1]{2,1,0:T(1,128)S(1)} async-done(((s32[8,1,1]{2,1,0:T(1,128)}), s32[8,1,1]{2,1,0:T(1,128)S(1)}, u32[]{:S(2)}, u32[]{:S(2)}) %all-to-all-start) | async-done | bytes 64 | tf_op jit(solution)/shard_map/all_to_all | solution.py:55
  23.1 1.0 gather_fusion
  24.1 1.6 select_bitcast_fusion
  25.7 3.6 %all-to-all-start.1 = ((bf16[2,8,512,128]{3,2,0,1:T(8,128)(2,1)}), bf16[2,8,512,128]{3,2,0,1:T(8,128)(2,1)S(1)}, u32[]{:S(2)}, u32[]{:S(2)}) async-start(bf16[2,8,512,128]{3,2,0,1:T(8,128)(2,1)} %select_bitcast_fusion), calls=%async_computation.1 | async-start | bytes 4194304 | tf_op jit(solution)/shard_map/all_to_all | solution.py:61
  29.7 46.7 %all-to-all-done.1 = bf16[2,8,512,128]{3,2,0,1:T(8,128)(2,1)S(1)} async-done(((bf16[2,8,512,128]{3,2,0,1:T(8,128)(2,1)}), bf16[2,8,512,128]{3,2,0,1:T(8,128)(2,1)S(1)}, u32[]{:S(2)}, u32[]{:S(2)}) %all-to-all-start.1) | async-done | bytes 2097184 | tf_op jit(solution)/shard_map/all_to_all | solution.py:61
  76.8 2.9 %gather_fusion.1 = bf16[14,2,512,128]{3,2,1,0:T(8,128)(2,1)} fusion(bf16[2,10,512,128]{3,2,1,0:T(8,128)(2,1)S(1)} %copy.52, s32[1024]{0:T(1024)S(1)} %pad_clamp_fusion), kind=kCustom, calls=%fused_computation.1 | custom fusion | bytes 7340088 | tf_op jit(solution)/shard_map/jit(_take)/gather | solution.py:72
  79.7 2.4 fusion.23
  82.2 2.3 slice_bitcast_fusion
  84.4 83.4 %while.10 = (s32[]{:T(128)}, bf16[2,512,4,128]{3,2,1,0:T(4,128)(2,1)S(1)}, bf16[2,7,512,128]{3,2,1,0:T(8,128)(2,1)}, pred[2,7]{1,0:T(4,128)(4,1)S(1)}, bf16[2,7,...) while((s32[]{:T(128)}, bf16[2,512,4,128]{3,2,1,0:T(4,128)(2,1)S(1)}, ...), condition=%wide.region_4.5_spmd, body=%wide.region_1.4_spmd.sunk | while | flops 3843289088 | bytes 109355664 | solution.py:74
  84.6 1.1 or_and_fusion.2
  85.8 13.3 %fusion.38 = (f32[4,512]{1,0:T(4,128)S(1)}, f32[7,512,512,4]{2,1,3,0:T(8,128)}) fusion(pred[512,7,512]{0,2,1:T(8,128)(4,1)S(1)} %or_and_fusion.2, bf16[1,512,4,128]{3,2,1,0:T(4,128)(2,1)S(1)} %constant_dynamic-slice_fusion.2, bf16[2,7,512,128]{3,2,1,0:T(8,128)(2,1)} %get-tuple-element.146, s32[]{:T(128)} %get-tuple-element.135), kind=kOutput, calls=%fused_computation.6.clone.1 | convolution fusion | flops 1901066240 | bytes 32645632 | tf_op jit(solution)/shard_map/while/body/eval_jaxpr/qgd,skd->gqsk/dot_general | solution.py:12
  99.2 12.9 %fusion.39 = f32[4,512]{1,0:T(4,128)S(1)} fusion(f32[7,512,512,4]{2,1,3,0:T(8,128)} %get-tuple-element.126, f32[4,512]{1,0:T(4,128)S(1)} %get-tuple-element.127, pred[512,7,512]{0,2,1:T(8,128)(4,1)S(1)} %or_and_fusion.2), kind=kLoop, calls=%fused_computation.4.clone.1 | loop fusion | flops 29358080 | bytes 31211520 | tf_op jit(solution)/shard_map/while/body/eval_jaxpr/reduce_sum | solution.py:23
  112.1 13.5 %fusion.40 = bf16[1,512,4,128]{1,3,2,0:T(8,128)(2,1)S(1)} fusion(f32[7,512,512,4]{2,1,3,0:T(8,128)} %get-tuple-element.126, f32[4,512]{1,0:T(4,128)S(1)} %get-tuple-element.127, pred[512,7,512]{0,2,1:T(8,128)(4,1)S(1)} %or_and_fusion.2, bf16[2,7,512,128]{3,2,1,0:T(8,128)(2,1)S(1)} %copy-done.1, s32[]{:T(128)} %get-tuple-element.135, ...), kind=kOutput, calls=%fused_computation.13.clone.1 | convolution fusion | flops 1908932608 | bytes 32653316 | tf_op jit(solution)/shard_map/while/body/eval_jaxpr/gqsk,skd->qgd/dot_general | solution.py:24
  126.3 1.1 or_and_fusion.2
  127.6 13.3 %fusion.38 = (f32[4,512]{1,0:T(4,128)S(1)}, f32[7,512,512,4]{2,1,3,0:T(8,128)}) fusion(pred[512,7,512]{0,2,1:T(8,128)(4,1)S(1)} %or_and_fusion.2, bf16[1,512,4,128]{3,2,1,0:T(4,128)(2,1)S(1)} %constant_dynamic-slice_fusion.2, bf16[2,7,512,128]{3,2,1,0:T(8,128)(2,1)} %get-tuple-element.146, s32[]{:T(128)} %get-tuple-element.135), kind=kOutput, calls=%fused_computation.6.clone.1 | convolution fusion | flops 1901066240 | bytes 32645632 | tf_op jit(solution)/shard_map/while/body/eval_jaxpr/qgd,skd->gqsk/dot_general | solution.py:12
  140.9 12.9 %fusion.39 = f32[4,512]{1,0:T(4,128)S(1)} fusion(f32[7,512,512,4]{2,1,3,0:T(8,128)} %get-tuple-element.126, f32[4,512]{1,0:T(4,128)S(1)} %get-tuple-element.127, pred[512,7,512]{0,2,1:T(8,128)(4,1)S(1)} %or_and_fusion.2), kind=kLoop, calls=%fused_computation.4.clone.1 | loop fusion | flops 29358080 | bytes 31211520 | tf_op jit(solution)/shard_map/while/body/eval_jaxpr/reduce_sum | solution.py:23
  153.8 13.5 %fusion.40 = bf16[1,512,4,128]{1,3,2,0:T(8,128)(2,1)S(1)} fusion(f32[7,512,512,4]{2,1,3,0:T(8,128)} %get-tuple-element.126, f32[4,512]{1,0:T(4,128)S(1)} %get-tuple-element.127, pred[512,7,512]{0,2,1:T(8,128)(4,1)S(1)} %or_and_fusion.2, bf16[2,7,512,128]{3,2,1,0:T(8,128)(2,1)S(1)} %copy-done.1, s32[]{:T(128)} %get-tuple-element.135, ...), kind=kOutput, calls=%fused_computation.13.clone.1 | convolution fusion | flops 1908932608 | bytes 32653316 | tf_op jit(solution)/shard_map/while/body/eval_jaxpr/gqsk,skd->qgd/dot_general | solution.py:24
  167.9 8.9 %convolution_convert_fusion = bf16[1024,4096]{1,0:T(8,128)(2,1)} fusion(bf16[512,4096]{1,0:T(8,128)(2,1)} %param.11, bf16[128,8,4,128]{3,2,1,0:T(4,128)(2,1)S(1)} %bitcast.113), kind=kOutput, calls=%fused_computation.28 | convolution fusion | flops 4299161600 | bytes 13631488 | tf_op jit(solution)/shard_map/dot_general | solution.py:81
  176.8 70.5 %reduce-scatter.2.cloned.1.call-done = bf16[256,4096]{1,0:T(8,128)(2,1)} async-done(((bf16[1024,4096]{1,0:T(8,128)(2,1)}), bf16[256,4096]{1,0:T(8,128)(2,1)}) %reduce-scatter.2.cloned.1.call-update) | async-done | bytes 2097168 | tf_op jit(solution)/shard_map/reduce_scatter | solution.py:83
  (48 shorter events, 3.1 us)
Async XLA Ops:
  9.0 13.8 %all-to-all-start = ((s32[8,1,1]{2,1,0:T(1,128)}), s32[8,1,1]{2,1,0:T(1,128)S(1)}, u32[]{:S(2)}, u32[]{:S(2)}) async-start(s32[8,1,1]{2,1,0:T(1,128)} %copy.49), calls=%async_computation | async-start | bytes 8192 | tf_op jit(solution)/shard_map/all_to_all | solution.py:55
  24.1 5.3 %copy-start.4 = (s32[2,1,6]{2,1,0:T(1,128)S(1)}, s32[2,1,6]{2,1,0:T(1,128)}, u32[]{:S(2)}) copy-start(s32[2,1,6]{2,1,0:T(1,128)} %param.10) | copy-start | bytes 148
  24.1 52.3 %copy-start.2 = (bf16[1024,1,128]{2,0,1:T(8,128)(2,1)S(1)}, bf16[1024,1,128]{2,0,1:T(8,128)(2,1)}, u32[]{:S(2)}) copy-start(bf16[1024,1,128]{2,0,1:T(8,128)(2,1)} %param.9) | copy-start | bytes 786436
  24.1 52.3 %copy-start.3 = (bf16[1024,1,128]{2,0,1:T(8,128)(2,1)S(1)}, bf16[1024,1,128]{2,0,1:T(8,128)(2,1)}, u32[]{:S(2)}) copy-start(bf16[1024,1,128]{2,0,1:T(8,128)(2,1)} %param.8) | copy-start | bytes 786436
  25.7 50.7 %all-to-all-start.1 = ((bf16[2,8,512,128]{3,2,0,1:T(8,128)(2,1)}), bf16[2,8,512,128]{3,2,0,1:T(8,128)(2,1)S(1)}, u32[]{:S(2)}, u32[]{:S(2)}) async-start(bf16[2,8,512,128]{3,2,0,1:T(8,128)(2,1)} %select_bitcast_fusion), calls=%async_computation.1 | async-start | bytes 4194304 | tf_op jit(solution)/shard_map/all_to_all | solution.py:61
  29.3 218.0 %reduce-scatter.2.cloned.1.call-start = ((), (), s32[]{:S(2)}) async-start(), calls=%async_computation.3 | async-start | bytes 10485760 | tf_op jit(solution)/shard_map/reduce_scatter | solution.py:83
  82.1 2.3 copy-start
  82.2 2.3 copy-start.5
  99.2 12.9 %copy-start.1 = (bf16[2,7,512,128]{3,2,1,0:T(8,128)(2,1)S(1)}, bf16[2,7,512,128]{3,2,1,0:T(8,128)(2,1)}, u32[]{:S(2)}) copy-start(bf16[2,7,512,128]{3,2,1,0:T(8,128)(2,1)} %get-tuple-element.144) | copy-start | bytes 5505028 | tf_op jit(solution)/shard_map/while
  140.9 12.9 %copy-start.1 = (bf16[2,7,512,128]{3,2,1,0:T(8,128)(2,1)S(1)}, bf16[2,7,512,128]{3,2,1,0:T(8,128)(2,1)}, u32[]{:S(2)}) copy-start(bf16[2,7,512,128]{3,2,1,0:T(8,128)(2,1)} %get-tuple-element.144) | copy-start | bytes 5505028 | tf_op jit(solution)/shard_map/while
Sparse Core Ops, SparseCore 0:
  176.9 70.3 reduce-scatter.1
where the time goes:
time: 255 us; the launch traced here: 254 us
  waiting for transfers between devices  123 us (48%)
  matrix products  62.6 us (25%)
  other arithmetic  34.7 us (14%)
  between operations  13.6 us (5%)
  starting transfers between devices  11 us (4%)
  local copies, waits for them, and re-layouts  9.59 us (4%)
    reduce_scatter x1, waiting for transfers between devices, body(): lax.psum_scatter(project().astype(jnp.bfloat16), 'head', scatter_dimensio...  70.5 us
    all_to_all x1, waiting for transfers between devices, body(): lax.all_to_all(packed, 'ctx', split_axis=1, concat_axis=1, tiled=True)  46.7 us
    dot_general x2, matrix products, attend_block(): jnp.einsum('gqsk,skd->qgd', weights.astype(jnp.bfloat16), value_block, pr...  27.1 us
    dot_general x2, matrix products, attend_block(): jnp.einsum('qgd,skd->gqsk', query_block, key_block, preferred_element_typ...  26.6 us
    reduce_sum x2, other arithmetic, attend_block(): totals = jnp.sum(weights, axis=(2, 3))  25.8 us
    dot_general x1, matrix products, project(): return jnp.dot(part_rows, final_mapping, preferred_element_type=jnp.float32)  8.92 us
    all_to_all x1, starting transfers between devices, body(): lax.all_to_all(coded.reshape(ctx_count, 1), 'ctx', split_axis=0, concat_a...  7.34 us
    all_to_all x1, waiting for transfers between devices, body(): lax.all_to_all(coded.reshape(ctx_count, 1), 'ctx', split_axis=0, concat_a...  5.33 us
  transfers between devices with their start and end apart: 3, of which 3 were waited for; matrix products, arithmetic and copies ran while one was open for 1% of the time, Pallas kernels for 0%

commit v1 on v0

v1 whole, which is shorter than its diff:
```python
import functools

import jax
import jax.numpy as jnp
from jax import lax
from jax.experimental import pallas as pl
from jax.experimental.pallas import tpu as pltpu
from jax.sharding import PartitionSpec as P

LOG2E = 1.4426950408889634


def attend_kernel(slots, live, q_ref, k_ref, v_ref, out_ref):
    block = pl.program_id(0)
    rows, depth = q_ref.shape
    count = slots.shape[1]
    factor = depth ** (-0.5) * LOG2E
    query = q_ref[...]
    peak = total = mixed = None
    for turn in range(count):
        slot = count - 1 if turn == 0 else turn - 1
        place = slots[block, slot]
        keys = k_ref[place]
        values = v_ref[place]
        scores = lax.dot_general(
            query, keys, (((1,), (1,)), ((), ())), preferred_element_type=jnp.float32
        )
        if turn == 0:
            row = lax.broadcasted_iota(jnp.int32, scores.shape, 0)
            column = lax.broadcasted_iota(jnp.int32, scores.shape, 1)
            scores = jnp.where(row >= column, scores, -jnp.inf)
            peak = jnp.max(scores, axis=1, keepdims=True)
            weights = jnp.exp2((scores - peak) * factor)
            total = jnp.sum(weights, axis=1, keepdims=True)
            mixed = jnp.dot(
                weights.astype(jnp.bfloat16), values, preferred_element_type=jnp.float32
            )
        else:
            alive = live[block, slot] > 0
            here = jnp.where(alive, jnp.max(scores, axis=1, keepdims=True), -jnp.inf)
            higher = jnp.maximum(peak, here)
            shift = jnp.where(alive, higher * factor, jnp.float32(1e30))
            weights = jnp.exp2(scores * factor - shift)
            keep = jnp.exp2((peak - higher) * factor)
            total = total * keep + jnp.sum(weights, axis=1, keepdims=True)
            mixed = mixed * keep + jnp.dot(
                weights.astype(jnp.bfloat16), values, preferred_element_type=jnp.float32
            )
            peak = higher
    out_ref[...] = (mixed / total).astype(jnp.bfloat16)


def attend(queries, key_pool, value_pool, slots, live):
    blocks = slots.shape[0]
    rows = queries.shape[0] // blocks
    depth = key_pool.shape[2]
    heads = queries.shape[1] // depth
    whole = pl.BlockSpec(key_pool.shape, lambda b, h, *_: (0, 0, 0))
    tile = pl.BlockSpec((rows, depth), lambda b, h, *_: (b, h))
    return pl.pallas_call(
        attend_kernel,
        out_shape=jax.ShapeDtypeStruct(queries.shape, jnp.bfloat16),
        grid_spec=pltpu.PrefetchScalarGridSpec(
            num_scalar_prefetch=2,
            grid=(blocks, heads),
            in_specs=[tile, whole, whole],
            out_specs=tile,
        ),
        compiler_params=pltpu.CompilerParams(vmem_limit_bytes=60 * 1024 * 1024),
        name="attend",
    )(slots, live, queries, key_pool, value_pool)


def body(queries, lookup_arrays, content_arrays, selection, final_mapping):
    ctx_count = lax.axis_size("ctx")
    position = lax.axis_index("ctx")
    blocks_here = selection.shape[0]
    tokens_here = queries.shape[0]
    block_size = tokens_here // blocks_here
    head_dim = queries.shape[2]
    stacked = jnp.stack(
        [
            lookup_arrays.reshape(blocks_here, block_size, head_dim),
            content_arrays.reshape(blocks_here, block_size, head_dim),
        ]
    )
    chosen = selection[:, 0, :]
    holder_list = chosen // blocks_here
    distant = holder_list <= position - 1
    peer_ids = jnp.arange(ctx_count, dtype=jnp.int32)
    last_id = ctx_count * blocks_here - 1
    matches = distant[:, :, None] & (holder_list[:, :, None] == peer_ids[None, None, :])
    wanted_ids = jnp.max(jnp.where(matches, chosen[:, :, None], -1), axis=(0, 1))
    coded = jnp.where(wanted_ids >= 0, last_id - wanted_ids, -1).astype(jnp.int32)
    received = lax.all_to_all(
        coded.reshape(ctx_count, 1), "ctx", split_axis=0, concat_axis=0, tiled=True
    ).reshape(ctx_count)
    requested = last_id - received
    local_index = jnp.clip(requested - position * blocks_here, 0, blocks_here - 1)
    packed = jnp.take(stacked, local_index, axis=1)
    arrived = lax.all_to_all(packed, "ctx", split_axis=1, concat_axis=1, tiled=True)
    block_pool = jnp.concatenate([stacked, arrived], axis=1)
    block_ids = position * blocks_here + jnp.arange(blocks_here, dtype=jnp.int32)
    slot_ids = jnp.concatenate([chosen, block_ids[:, None]], axis=1)
    live = (slot_ids != block_ids[:, None]).astype(jnp.int32)
    slot_owner = slot_ids // blocks_here
    pool_index = jnp.where(
        slot_owner == position, slot_ids - position * blocks_here, blocks_here + slot_owner
    )
    flat_rows = attend(
        queries.reshape(tokens_here, -1), block_pool[0], block_pool[1], pool_index, live
    )
    terms = jnp.dot(flat_rows, final_mapping, preferred_element_type=jnp.float32)
    summed = lax.psum_scatter(
        terms.astype(jnp.bfloat16), "head", scatter_dimension=0, tiled=True
    ).astype(jnp.float32)
    return summed.astype(jnp.bfloat16)


def solution(mesh):
    in_specs = (
        P("ctx", "head", None),
        P("ctx", "head", None),
        P("ctx", "head", None),
        P("ctx", "head", None),
        P("head", None),
    )
    out_specs = P(("ctx", "head"), None)
    return jax.shard_map(body, mesh=mesh, in_specs=in_specs, out_specs=out_specs, check_vma=False)
```

time: 255 us -> 196 us (0.77)
  matrix products: 62.6 us -> 10.2 us
  Pallas kernels: 0 us -> 28.6 us
  other arithmetic: 34.7 us -> 6.23 us
  local copies, waits for them, and re-layouts: 9.59 us -> 5.45 us
  waiting for transfers between devices: 123 us -> 120 us
    dot_general x5 -> x1, matrix products: 62.6 us -> 10.2 us  [body(): jnp.dot(flat_rows, final_mapping, preferred_element_type=jnp.float32)]
    pallas_call x0 -> x1, Pallas kernels: none -> 28.6 us  [attend(): pl.pallas_call(attend_kernel, out_shape=jax.ShapeDtypeStruct(queries.shap...]
    reduce_sum x2 -> x0, other arithmetic: 25.8 us -> none  [attend_block(): totals = jnp.sum(weights, axis=(2, 3))]
    gather x1 -> x0, local copies, waits for them, and re-layouts: 2.86 us -> none  [body(): selected = jnp.take(block_pool, pool_index, axis=1)]
  transfers between devices with their start and end apart: 3 -> 3, of which waited for: 3 -> 3; matrix products, arithmetic and copies ran while one was open for 1% -> 2% of each run, Pallas kernels for 0% -> 0%
where the time goes in v1:
time: 196 us
  waiting for transfers between devices  120 us (61%)
  Pallas kernels  28.6 us (15%)
  between operations  13.5 us (7%)
  starting transfers between devices  11.1 us (6%)
  matrix products  10.2 us (5%)
  other arithmetic  6.23 us (3%)
  local copies, waits for them, and re-layouts  5.45 us (3%)
    reduce_scatter x1, waiting for transfers between devices, body(): lax.psum_scatter(terms.astype(jnp.bfloat16), 'head', scatter_dimension=0,...  70.5 us
    all_to_all x1, waiting for transfers between devices, body(): lax.all_to_all(packed, 'ctx', split_axis=1, concat_axis=1, tiled=True)  44.5 us
    pallas_call x1, Pallas kernels, attend(): pl.pallas_call(attend_kernel, out_shape=jax.ShapeDtypeStruct(queries.shap...  28.6 us
    dot_general x1, matrix products, body(): jnp.dot(flat_rows, final_mapping, preferred_element_type=jnp.float32)  10.2 us
    all_to_all x1, starting transfers between devices, body(): lax.all_to_all(coded.reshape(ctx_count, 1), 'ctx', split_axis=0, concat_a...  7.34 us
    all_to_all x1, waiting for transfers between devices, body(): lax.all_to_all(coded.reshape(ctx_count, 1), 'ctx', split_axis=0, concat_a...  5.38 us
  transfers between devices with their start and end apart: 3, of which 3 were waited for; matrix products, arithmetic and copies ran while one was open for 2% of the time, Pallas kernels for 0%

profile of v1, /device:TPU:0, one launch (start us, length us, event | category | flops | bytes accessed | tf_op | source)
XLA Modules:
  0.0 195.5 jit_solution(6489676881825868004)
XLA Ops:
  6.5 0.8 copy.13
  7.3 0.7 broadcast_compare_fusion
  8.0 0.1 copy.11
  8.1 0.1 copy.12
  8.2 0.1 fusion
  8.3 0.7 copy.14
  9.0 7.3 %all-to-all-start = ((s32[8,1,1]{2,1,0:T(1,128)}), s32[8,1,1]{2,1,0:T(1,128)S(1)}, u32[]{:S(2)}, u32[]{:S(2)}) async-start(s32[8,1,1]{2,1,0:T(1,128)} %copy.14), calls=%async_computation | async-start | bytes 8192 | tf_op jit(solution)/shard_map/all_to_all | solution.py:95
  16.3 1.1 pad_maximum_fusion.1
  17.4 5.4 %all-to-all-done = s32[8,1,1]{2,1,0:T(1,128)S(1)} async-done(((s32[8,1,1]{2,1,0:T(1,128)}), s32[8,1,1]{2,1,0:T(1,128)S(1)}, u32[]{:S(2)}, u32[]{:S(2)}) %all-to-all-start) | async-done | bytes 64 | tf_op jit(solution)/shard_map/all_to_all | solution.py:95
  22.8 0.2 clamp_reduce_fusion
  23.1 1.0 gather_fusion
  24.0 1.6 select_bitcast_fusion
  25.6 3.7 %all-to-all-start.1 = ((bf16[2,8,512,128]{3,2,0,1:T(8,128)(2,1)}), bf16[2,8,512,128]{3,2,0,1:T(8,128)(2,1)S(1)}, u32[]{:S(2)}, u32[]{:S(2)}) async-start(bf16[2,8,512,128]{3,2,0,1:T(8,128)(2,1)} %select_bitcast_fusion), calls=%async_computation.1 | async-start | bytes 4194304 | tf_op jit(solution)/shard_map/all_to_all | solution.py:101
  29.4 0.0 reduce-scatter.2.cloned.1.call-start
  29.4 1.2 copy.20
  30.6 0.7 compare_select_fusion.3.slots
  31.3 0.7 compare_convert_fusion.live
  31.9 44.5 %all-to-all-done.1 = bf16[2,8,512,128]{3,2,0,1:T(8,128)(2,1)S(1)} async-done(((bf16[2,8,512,128]{3,2,0,1:T(8,128)(2,1)}), bf16[2,8,512,128]{3,2,0,1:T(8,128)(2,1)S(1)}, u32[]{:S(2)}, u32[]{:S(2)}) %all-to-all-start.1) | async-done | bytes 2097184 | tf_op jit(solution)/shard_map/all_to_all | solution.py:101
  76.4 1.2 pad_maximum_fusion
  77.6 1.7 slice_bitcast_fusion
  79.3 28.6 %attend.1 = bf16[1024,512]{1,0:T(8,128)(2,1)} custom-call(s32[2,7]{1,0:T(2,128)} %compare_select_fusion.3.slots, s32[2,7]{1,0:T(2,128)} %compare_convert_fusion.live, bf16[1024,512]{1,0:T(8,128)(2,1)} %bitcast.21, bf16[10,512,128]{2,1,0:T(8,128)(2,1)} %get-tuple-element.8.k_ref, bf16[10,512,128]{2,1,0:T(8,128)(2,1)} %get-tuple-element.7.v_ref), custom_call_target="tpu_custom_call" | custom-call | tf_op jit(solution)/shard_map/attend/pallas_call | solution.py:60
  107.8 10.2 %convolution_convert_fusion = bf16[1024,4096]{1,0:T(8,128)(2,1)} fusion(bf16[1024,512]{1,0:T(8,128)(2,1)} %attend.1, bf16[512,4096]{1,0:T(8,128)(2,1)} %param.9), kind=kOutput, calls=%fused_computation.1 | convolution fusion | flops 4299161600 | bytes 13631488 | tf_op jit(solution)/shard_map/dot_general | solution.py:113
  118.1 0.0 reduce-scatter.2.cloned.1.call-update
  118.1 70.5 %reduce-scatter.2.cloned.1.call-done = bf16[256,4096]{1,0:T(8,128)(2,1)} async-done(((bf16[1024,4096]{1,0:T(8,128)(2,1)}), bf16[256,4096]{1,0:T(8,128)(2,1)}) %reduce-scatter.2.cloned.1.call-update) | async-done | bytes 2097168 | tf_op jit(solution)/shard_map/reduce_scatter | solution.py:114
  (12 shorter events, 0.0 us)
Async XLA Ops:
  9.0 13.8 %all-to-all-start = ((s32[8,1,1]{2,1,0:T(1,128)}), s32[8,1,1]{2,1,0:T(1,128)S(1)}, u32[]{:S(2)}, u32[]{:S(2)}) async-start(s32[8,1,1]{2,1,0:T(1,128)} %copy.14), calls=%async_computation | async-start | bytes 8192 | tf_op jit(solution)/shard_map/all_to_all | solution.py:95
  25.6 3.8 %copy-start = (bf16[1024,4,128]{2,1,0:T(4,128)(2,1)S(1)}, bf16[1024,4,128]{2,1,0:T(4,128)(2,1)}, u32[]{:S(2)}) copy-start(bf16[1024,4,128]{2,1,0:T(4,128)(2,1)} %param.5) | copy-start | bytes 3145732
  25.6 5.0 %copy-start.2 = (s32[2,1,6]{2,1,0:T(1,128)S(1)}, s32[2,1,6]{2,1,0:T(1,128)}, u32[]{:S(2)}) copy-start(s32[2,1,6]{2,1,0:T(1,128)} %param.8) | copy-start | bytes 148
  25.6 50.8 %copy-start.1 = (bf16[1024,1,128]{2,0,1:T(8,128)(2,1)S(1)}, bf16[1024,1,128]{2,0,1:T(8,128)(2,1)}, u32[]{:S(2)}) copy-start(bf16[1024,1,128]{2,0,1:T(8,128)(2,1)} %param.7) | copy-start | bytes 786436
  25.6 50.8 %all-to-all-start.1 = ((bf16[2,8,512,128]{3,2,0,1:T(8,128)(2,1)}), bf16[2,8,512,128]{3,2,0,1:T(8,128)(2,1)S(1)}, u32[]{:S(2)}, u32[]{:S(2)}) async-start(bf16[2,8,512,128]{3,2,0,1:T(8,128)(2,1)} %select_bitcast_fusion), calls=%async_computation.1 | async-start | bytes 4194304 | tf_op jit(solution)/shard_map/all_to_all | solution.py:101
  29.4 159.3 %reduce-scatter.2.cloned.1.call-start = ((), (), s32[]{:S(2)}) async-start(), calls=%async_computation.3 | async-start | bytes 10485760 | tf_op jit(solution)/shard_map/reduce_scatter | solution.py:114
Sparse Core Ops, SparseCore 0:
  118.2 70.3 reduce-scatter.1
